TPU v7x, 32 devices: a whole 2x2x4 slice. The times are simulated.
32 devices in a mesh: dp: 8 (over z, y), group: 4 (over x, core).
Axes of the slice: x: 2, y: 2, z: 4, core: 2. Of those that a mesh axis runs over, the one named last changes fastest.
Arguments:
- keys: int32 [16384], P(('dp', 'group')), may hold values from 0 to 1073741823
- cut: int32 [1], replicated, may hold values from 256 to 1023
- owner: int32 [16384, 1], P(('dp', 'group')), may hold values from 0 to 7; in each aligned block of 512 rows (0 to 511, 512 to 1023, ...) at most 128 rows name the same one
- tokens: int32 [16384, 2048], P(('dp', 'group')), may hold values from 0 to 128255
Outputs:
- histogram: int32 [4096], replicated
- packed_rows: int32 [32768, 2048], P(('dp', 'group'))
- packed_weights: float32 [32768], P(('dp', 'group'))
Inputs may be any that keep to these rules, and one draw needn't show every extreme that they name: Among the examples of one device, at most 128 have the same owner, and some owner has exactly 128.
All inputs are finite; a program needn't handle non-finite values.
Results may differ from a plain program's by a relative error of at most 0.0003.
Values sent between devices are 32-bit elements; how exact they have to be, the bound alone decides.
A program may use at most 128 MiB of HBM per device.

v0:
```python
import jax
import jax.numpy as jnp
from jax import lax
from jax.sharding import PartitionSpec as P

BINS = 4096
BIN_WIDTH = 262144


def body(keys, cut, owner, tokens):
    examples = keys.shape[0]
    width = tokens.shape[1]
    n_owner = lax.axis_size("dp")
    n_member = lax.axis_size("group")
    slots = 2 * examples // (n_owner * n_member)
    capacity = 2 * examples
    bins_of = keys // BIN_WIDTH
    local_hist = jnp.zeros((BINS,), jnp.float32).at[bins_of].add(1.0)
    kept = bins_of >= cut[0]
    dest = owner[:, 0]
    onehot = (
        (dest[:, None] == jnp.arange(n_owner, dtype=jnp.int32)[None, :]) & kept[:, None]
    ).astype(jnp.int32)
    counts = jnp.sum(onehot, axis=0).astype(jnp.float32)
    table = lax.all_gather(counts[None, :], ("dp", "group"), axis=0, tiled=True)
    position = lax.axis_index(("dp", "group"))
    below = jnp.arange(table.shape[0], dtype=jnp.int32) < position
    before = jnp.sum(jnp.where(below[:, None], table, 0.0), axis=0)
    hist = lax.psum(local_hist, ("dp", "group"))
    running = jnp.cumsum(onehot, axis=0) - onehot
    local_rank = jnp.sum(running * onehot, axis=1)
    offset = jnp.sum(before.astype(jnp.int32)[None, :] * onehot, axis=1)
    rank = offset + local_rank
    member = rank % n_member
    outside = n_owner * n_member * slots
    position_send = jnp.where(
        kept, (dest * n_member + member) * slots + local_rank // n_member, outside
    )
    send_rows = jnp.zeros((outside, width), jnp.int32).at[position_send].set(tokens, mode="drop")
    details = jnp.stack([rank // n_member, keys], axis=1)
    send_meta = jnp.full((outside, 2), -1, jnp.int32).at[position_send].set(details, mode="drop")
    send_rows = send_rows.reshape(n_owner, n_member, slots, width)
    send_meta = send_meta.reshape(n_owner, n_member, slots, 2)
    got_rows, got_meta = (
        lax.all_to_all(
            lax.all_to_all(send_rows, "dp", split_axis=0, concat_axis=0, tiled=True),
            "group",
            split_axis=1,
            concat_axis=1,
            tiled=True,
        ),
        lax.all_to_all(
            lax.all_to_all(send_meta, "dp", split_axis=0, concat_axis=0, tiled=True),
            "group",
            split_axis=1,
            concat_axis=1,
            tiled=True,
        ),
    )
    got_rows = got_rows.reshape(-1, width)
    got_meta = got_meta.reshape(-1, 2)
    slot = got_meta[:, 0]
    valid = slot >= 0
    target = jnp.where(valid, slot, capacity)
    suffix = jnp.cumsum(hist[::-1])[::-1]
    total = jnp.maximum(suffix[cut[0]], 1.0)
    got_bins = jnp.clip(got_meta[:, 1] // BIN_WIDTH, 0, BINS - 1)
    weight = jnp.where(valid, suffix[got_bins] / total, 0.0)
    packed_rows = jnp.zeros((capacity, width), jnp.int32).at[target].set(got_rows, mode="drop")
    packed_weights = jnp.zeros((capacity,), jnp.float32).at[target].set(weight, mode="drop")
    return (hist.astype(jnp.int32), packed_rows, packed_weights)


def solution(mesh):
    placed = (P(("dp", "group")), P(), P(("dp", "group"), None), P(("dp", "group"), None))
    return jax.shard_map(
        body,
        mesh=mesh,
        in_specs=placed,
        out_specs=(P(), P(("dp", "group"), None), P(("dp", "group"))),
        check_vma=False,
    )
```

profile of v0, /device:TPU:0, one launch (start us, length us, event | category | flops | bytes accessed | tf_op | source)
XLA Modules:
  0.0 387.2 jit_solution(11714940786831163853)
XLA Ops:
  1.3 0.7 broadcast_compare_fusion
  2.0 0.8 convert_reduce_fusion
  2.8 3.3 scatter_custom_fusion
  6.2 42.1 %all-reduce.1 = (f32[4096]{0:T(1024)S(1)}, f32[256]{0:T(256)S(1)}) all-reduce(f32[4096]{0:T(1024)S(1)} %scatter_custom_fusion, f32[256]{0:T(256)S(1)} %convert_dynamic-update-slice_fusion), channel_id=1, replica_groups=mesh['dp'=8,'group'=4] {'dp','group'}, use_global_device_ids=true, to_apply=%region_1.2 | all-reduce | flops 4352 | bytes 34816 | tf_op jit(solution)/shard_map/psum | solution.py:29
  48.5 0.7 fusion.10
  49.2 1.1 reduce-window.15
  50.3 0.2 slice_reduce_fusion.1
  50.6 0.8 select_reduce_fusion
  51.4 0.7 compare_select_fusion.6
  52.1 0.7 pad_add_fusion
  52.9 1.8 scatter_custom_fusion.1
  54.8 0.3 copy.20
  55.0 0.7 reshape.203
  55.7 5.3 %all-to-all-start = ((s32[8,1,256]{2,1,0:T(1,128)}), s32[8,1,256]{2,1,0:T(1,128)S(1)}, u32[]{:S(2)}, u32[]{:S(2)}) async-start(s32[8,1,256]{2,1,0:T(1,128)} %reshape.203), calls=%async_computation | async-start | bytes 16384 | tf_op jit(solution)/shard_map/all_to_all | solution.py:53
  61.1 8.6 %scatter_custom_fusion.2 = s32[1024,2048]{1,0:T(8,128)} fusion(s32[512]{0:T(512)S(1)} %get-tuple-element.7, s32[512,2048]{1,0:T(8,128)} %param.7, s32[]{:T(128)} %constant.83.clone.1), kind=kCustom, calls=%fused_computation.8 | custom fusion | bytes 8389120 | tf_op jit(solution)/shard_map/scatter | solution.py:39
  69.7 6.0 %all-to-all-start.2 = ((s32[8,4,32,2048]{3,2,1,0:T(8,128)}), s32[8,4,32,2048]{3,2,1,0:T(8,128)}, u32[]{:S(2)}, u32[]{:S(2)}) async-start(s32[8,4,32,2048]{3,2,1,0:T(8,128)} %bitcast.35), calls=%async_computation.2 | async-start | bytes 16777216 | tf_op jit(solution)/shard_map/all_to_all | solution.py:46
  75.7 0.5 broadcast.157
  76.2 0.6 reduce.6
  76.9 0.7 reshape.205
  77.5 179.0 %all-to-all-done.2 = s32[8,4,32,2048]{3,2,1,0:T(8,128)} async-done(((s32[8,4,32,2048]{3,2,1,0:T(8,128)}), s32[8,4,32,2048]{3,2,1,0:T(8,128)}, u32[]{:S(2)}, u32[]{:S(2)}) %all-to-all-start.2) | async-done | bytes 8388640 | tf_op jit(solution)/shard_map/all_to_all | solution.py:46
  256.5 3.2 all-to-all-start.1
  259.8 7.9 %copy.23 = s32[8,4,32,2048]{3,2,0,1:T(8,128)} copy(s32[8,4,32,2048]{3,2,1,0:T(8,128)} %all-to-all-done.2) | data formatting | bytes 16777216 | tf_op jit(solution)/shard_map/all_to_all | solution.py:46
  267.7 5.7 %all-to-all-start.3 = ((s32[8,4,32,2048]{3,2,0,1:T(8,128)}), s32[8,4,32,2048]{3,2,0,1:T(8,128)}, u32[]{:S(2)}, u32[]{:S(2)}) async-start(s32[8,4,32,2048]{3,2,0,1:T(8,128)} %copy.23), calls=%async_computation.3 | async-start | bytes 16777216 | tf_op jit(solution)/shard_map/all_to_all | solution.py:45
  273.4 0.6 convert_element_type.30
  274.0 0.3 reduce-window.19
  274.7 0.6 dynamic_slice.3
  276.0 0.6 reduce.7
  276.8 6.2 %gather_fusion = f32[1024]{0:T(1024)S(1)} fusion(f32[4096]{0:T(1024)S(1)} %rev.7, s32[1024]{0:T(1024)S(1)} %broadcast_clamp_fusion), kind=kCustom, calls=%fused_computation | custom fusion | bytes 12288 | tf_op jit(solution)/shard_map/gather | solution.py:68
  283.0 4.9 %scatter_custom_fusion.4 = f32[1024]{0:T(1024)} fusion(s32[1024]{0:T(1024)S(1)} %bitcast.51, f32[1024]{0:T(1024)S(1)} %divide_select_fusion, f32[]{:T(128)} %constant.81.clone.1), kind=kCustom, calls=%fused_computation.63 | custom fusion | bytes 4100 | tf_op jit(solution)/shard_map/scatter | solution.py:70
  287.9 78.6 %all-to-all-done.3 = s32[8,4,32,2048]{3,2,0,1:T(8,128)} async-done(((s32[8,4,32,2048]{3,2,0,1:T(8,128)}), s32[8,4,32,2048]{3,2,0,1:T(8,128)}, u32[]{:S(2)}, u32[]{:S(2)}) %all-to-all-start.3) | async-done | bytes 8388640 | tf_op jit(solution)/shard_map/all_to_all | solution.py:45
  366.5 7.7 %copy.24 = s32[8,4,32,2048]{3,2,1,0:T(8,128)} copy(s32[8,4,32,2048]{3,2,0,1:T(8,128)} %all-to-all-done.3) | data formatting | bytes 16777216 | tf_op jit(solution)/shard_map/all_to_all | solution.py:45
  374.2 13.0 %scatter_custom_fusion.3 = s32[1024,2048]{1,0:T(8,128)} fusion(s32[1024]{0:T(1024)S(1)} %bitcast.52, s32[1024,2048]{1,0:T(8,128)} %bitcast.36, s32[]{:T(128)} %constant.83.clone.1), kind=kCustom, calls=%fused_computation.6 | custom fusion | bytes 8389120 | tf_op jit(solution)/shard_map/scatter | solution.py:69
  (29 shorter events, 1.3 us)
Async XLA Ops:
  55.7 13.9 %all-to-all-start = ((s32[8,1,256]{2,1,0:T(1,128)}), s32[8,1,256]{2,1,0:T(1,128)S(1)}, u32[]{:S(2)}, u32[]{:S(2)}) async-start(s32[8,1,256]{2,1,0:T(1,128)} %reshape.203), calls=%async_computation | async-start | bytes 16384 | tf_op jit(solution)/shard_map/all_to_all | solution.py:53
  69.7 186.9 %all-to-all-start.2 = ((s32[8,4,32,2048]{3,2,1,0:T(8,128)}), s32[8,4,32,2048]{3,2,1,0:T(8,128)}, u32[]{:S(2)}, u32[]{:S(2)}) async-start(s32[8,4,32,2048]{3,2,1,0:T(8,128)} %bitcast.35), calls=%async_computation.2 | async-start | bytes 16777216 | tf_op jit(solution)/shard_map/all_to_all | solution.py:46
  256.5 11.1 %all-to-all-start.1 = ((s32[4,1,512]{2,1,0:T(1,128)}), s32[4,1,512]{2,1,0:T(1,128)S(1)}, u32[]{:S(2)}, u32[]{:S(2)}) async-start(s32[4,1,512]{2,1,0:T(1,128)} %reshape.205), calls=%async_computation.1 | async-start | bytes 16384 | tf_op jit(solution)/shard_map/all_to_all | solution.py:52
  267.7 98.8 %all-to-all-start.3 = ((s32[8,4,32,2048]{3,2,0,1:T(8,128)}), s32[8,4,32,2048]{3,2,0,1:T(8,128)}, u32[]{:S(2)}, u32[]{:S(2)}) async-start(s32[8,4,32,2048]{3,2,0,1:T(8,128)} %copy.23), calls=%async_computation.3 | async-start | bytes 16777216 | tf_op jit(solution)/shard_map/all_to_all | solution.py:45
where the time goes:
time: 388 us; the launch traced here: 387 us
  waiting for transfers between devices  258 us (66%)
  local copies, waits for them, and re-layouts  53.9 us (14%)
  blocking collectives  42.1 us (11%)
  starting transfers between devices  20.2 us (5%)
  other arithmetic  11.3 us (3%)
    all_to_all x1, waiting for transfers between devices, body(): lax.all_to_all(send_rows, 'dp', split_axis=0, concat_axis=0, tiled=True)  179 us
    all_to_all x1, waiting for transfers between devices, body(): lax.all_to_all(lax.all_to_all(send_rows, 'dp', split_axis=0, concat_axis=...  78.6 us
    psum x1, blocking collectives, body(): hist = lax.psum(local_hist, ('dp', 'group'))  42.1 us
    scatter x1, local copies, waits for them, and re-layouts, body(): jnp.zeros((capacity, width), jnp.int32).at[target]  13 us
    scatter x1, local copies, waits for them, and re-layouts, body(): jnp.zeros((outside, width), jnp.int32).at[position_send]  8.6 us
    all_to_all x1, local copies, waits for them, and re-layouts, body(): lax.all_to_all(send_rows, 'dp', split_axis=0, concat_axis=0, tiled=True)  7.89 us
  transfers between devices with their start and end apart: 4, of which 2 were waited for; matrix products, arithmetic and copies ran while one was open for 8% of the time, Pallas kernels for 0%

commit v1 on v0

--- a/solution.py
+++ b/solution.py
@@ -26,7 +26,7 @@
     position = lax.axis_index(("dp", "group"))
     below = jnp.arange(table.shape[0], dtype=jnp.int32) < position
     before = jnp.sum(jnp.where(below[:, None], table, 0.0), axis=0)
-    hist = lax.psum(local_hist, ("dp", "group"))
+    hist = jnp.sum(lax.all_gather(local_hist, ("dp", "group")), 0)
     running = jnp.cumsum(onehot, axis=0) - onehot
     local_rank = jnp.sum(running * onehot, axis=1)
     offset = jnp.sum(before.astype(jnp.int32)[None, :] * onehot, axis=1)

time: 388 us -> 432 us (1.11)
  blocking collectives: 42.1 us -> 164 us
  waiting for transfers between devices: 258 us -> 179 us
    all_gather x0 -> x1, blocking collectives: none -> 122 us  [body(): hist = jnp.sum(lax.all_gather(local_hist, ('dp', 'group')), 0)]
    all_to_all x1, waiting for transfers between devices: 78.6 us -> 0.01 us  [body(): lax.all_to_all(lax.all_to_all(send_rows, 'dp', split_axis=0, concat_axis=...]
    psum x1 -> x0, blocking collectives: 42.1 us -> none  [body(): hist = lax.psum(local_hist, ('dp', 'group'))]
    unnamed x0 -> x1, blocking collectives: none -> 41.9 us
  transfers between devices with their start and end apart: 4 -> 4, of which waited for: 2 -> 1; matrix products, arithmetic and copies ran while one was open for 8% -> 8% of each run, Pallas kernels for 0% -> 0%
where the time goes in v1:
time: 432 us; the launch traced here: 431 us
  waiting for transfers between devices  179 us (41%)
  blocking collectives  164 us (38%)
  local copies, waits for them, and re-layouts  54 us (12%)
  starting transfers between devices  20.2 us (5%)
  other arithmetic  11.3 us (3%)
    all_to_all x1, waiting for transfers between devices, body(): lax.all_to_all(send_rows, 'dp', split_axis=0, concat_axis=0, tiled=True)  179 us
    all_gather x1, blocking collectives, body(): hist = jnp.sum(lax.all_gather(local_hist, ('dp', 'group')), 0)  122 us
    unnamed x1, blocking collectives  41.9 us
    scatter x1, local copies, waits for them, and re-layouts, body(): jnp.zeros((capacity, width), jnp.int32).at[target]  13 us
  transfers between devices with their start and end apart: 4, of which 1 were waited for; matrix products, arithmetic and copies ran while one was open for 8% of the time, Pallas kernels for 0%

profile of v1, /device:TPU:0, one launch (start us, length us, event | category | flops | bytes accessed | tf_op | source)
XLA Modules:
  0.0 430.8 jit_solution(2945740407947892639)
XLA Ops:
  1.3 0.7 broadcast_compare_fusion
  2.0 0.8 convert_reduce_fusion
  2.9 41.9 %all-reduce = f32[256]{0:T(256)S(1)} all-reduce(f32[256]{0:T(256)S(1)} %convert_dynamic-update-slice_fusion), channel_id=3, replica_groups=mesh['dp'=8,'group'=4] {'dp','group'}, use_global_device_ids=true, to_apply=%add | all-reduce | flops 256 | bytes 2048
  45.0 0.7 fusion.10
  45.7 1.1 reduce-window.15
  46.8 0.2 slice_reduce_fusion.1
  47.1 0.8 select_reduce_fusion
  47.9 0.7 compare_select_fusion.6
  48.6 0.7 pad_add_fusion
  49.4 1.8 scatter_custom_fusion.1
  51.3 0.3 copy.26
  51.5 0.7 reshape.204
  52.3 5.3 %all-to-all-start = ((s32[8,1,256]{2,1,0:T(1,128)}), s32[8,1,256]{2,1,0:T(1,128)S(1)}, u32[]{:S(2)}, u32[]{:S(2)}) async-start(s32[8,1,256]{2,1,0:T(1,128)} %reshape.204), calls=%async_computation | async-start | bytes 16384 | tf_op jit(solution)/shard_map/all_to_all | solution.py:53
  57.6 8.6 %scatter_custom_fusion.2 = s32[1024,2048]{1,0:T(8,128)} fusion(s32[512]{0:T(512)S(1)} %get-tuple-element.5, s32[512,2048]{1,0:T(8,128)} %param.7, s32[]{:T(128)} %constant.83.clone.1), kind=kCustom, calls=%fused_computation.8 | custom fusion | bytes 8389120 | tf_op jit(solution)/shard_map/scatter | solution.py:39
  66.2 6.0 %all-to-all-start.2 = ((s32[8,4,32,2048]{3,2,1,0:T(8,128)}), s32[8,4,32,2048]{3,2,1,0:T(8,128)}, u32[]{:S(2)}, u32[]{:S(2)}) async-start(s32[8,4,32,2048]{3,2,1,0:T(8,128)} %bitcast.31), calls=%async_computation.2 | async-start | bytes 16777216 | tf_op jit(solution)/shard_map/all_to_all | solution.py:46
  72.2 0.5 broadcast.157
  72.6 0.6 reduce.6
  73.3 0.7 reshape.206
  74.0 179.0 %all-to-all-done.2 = s32[8,4,32,2048]{3,2,1,0:T(8,128)} async-done(((s32[8,4,32,2048]{3,2,1,0:T(8,128)}), s32[8,4,32,2048]{3,2,1,0:T(8,128)}, u32[]{:S(2)}, u32[]{:S(2)}) %all-to-all-start.2) | async-done | bytes 8388640 | tf_op jit(solution)/shard_map/all_to_all | solution.py:46
  253.0 3.2 all-to-all-start.1
  256.3 7.9 %copy.29 = s32[8,4,32,2048]{3,2,0,1:T(8,128)} copy(s32[8,4,32,2048]{3,2,1,0:T(8,128)} %all-to-all-done.2) | data formatting | bytes 16777216 | tf_op jit(solution)/shard_map/all_to_all | solution.py:46
  264.2 5.7 %all-to-all-start.3 = ((s32[8,4,32,2048]{3,2,0,1:T(8,128)}), s32[8,4,32,2048]{3,2,0,1:T(8,128)}, u32[]{:S(2)}, u32[]{:S(2)}) async-start(s32[8,4,32,2048]{3,2,0,1:T(8,128)} %copy.29), calls=%async_computation.3 | async-start | bytes 16777216 | tf_op jit(solution)/shard_map/all_to_all | solution.py:45
  269.9 3.3 scatter_custom_fusion
  273.1 122.2 %all-gather = f32[131072]{0:T(1024)S(1)} all-gather(f32[4096]{0:T(1024)S(1)} %scatter_custom_fusion), channel_id=2, replica_groups=mesh['dp'=8,'group'=4] {'dp','group'}, dimensions={0}, use_global_device_ids=true | all-gather | bytes 540672 | tf_op jit(solution)/shard_map/all_gather | solution.py:29
  395.6 0.6 convert_element_type.30
  396.2 0.3 reduce-window.19
  396.9 0.6 dynamic_slice.3
  398.1 0.6 reduce.7
  399.0 6.2 %gather_fusion = f32[1024]{0:T(1024)S(1)} fusion(f32[4096]{0:T(1024)S(1)} %rev.7, s32[1024]{0:T(1024)S(1)} %broadcast_clamp_fusion), kind=kCustom, calls=%fused_computation | custom fusion | bytes 12288 | tf_op jit(solution)/shard_map/gather | solution.py:68
  405.2 4.9 %scatter_custom_fusion.4 = f32[1024]{0:T(1024)} fusion(s32[1024]{0:T(1024)S(1)} %bitcast.47, f32[1024]{0:T(1024)S(1)} %divide_select_fusion, f32[]{:T(128)} %constant.81.clone.1), kind=kCustom, calls=%fused_computation.63 | custom fusion | bytes 4100 | tf_op jit(solution)/shard_map/scatter | solution.py:70
  410.0 7.7 %copy.30 = s32[8,4,32,2048]{3,2,1,0:T(8,128)} copy(s32[8,4,32,2048]{3,2,0,1:T(8,128)} %all-to-all-done.3) | data formatting | bytes 16777216 | tf_op jit(solution)/shard_map/all_to_all | solution.py:45
  417.7 13.0 %scatter_custom_fusion.3 = s32[1024,2048]{1,0:T(8,128)} fusion(s32[1024]{0:T(1024)S(1)} %bitcast.48, s32[1024,2048]{1,0:T(8,128)} %bitcast.32, s32[]{:T(128)} %constant.83.clone.1), kind=kCustom, calls=%fused_computation.6 | custom fusion | bytes 8389120 | tf_op jit(solution)/shard_map/scatter | solution.py:69
  (32 shorter events, 1.5 us)
Async XLA Ops:
  52.3 13.9 %all-to-all-start = ((s32[8,1,256]{2,1,0:T(1,128)}), s32[8,1,256]{2,1,0:T(1,128)S(1)}, u32[]{:S(2)}, u32[]{:S(2)}) async-start(s32[8,1,256]{2,1,0:T(1,128)} %reshape.204), calls=%async_computation | async-start | bytes 16384 | tf_op jit(solution)/shard_map/all_to_all | solution.py:53
  66.2 186.9 %all-to-all-start.2 = ((s32[8,4,32,2048]{3,2,1,0:T(8,128)}), s32[8,4,32,2048]{3,2,1,0:T(8,128)}, u32[]{:S(2)}, u32[]{:S(2)}) async-start(s32[8,4,32,2048]{3,2,1,0:T(8,128)} %bitcast.31), calls=%async_computation.2 | async-start | bytes 16777216 | tf_op jit(solution)/shard_map/all_to_all | solution.py:46
  253.0 11.1 %all-to-all-start.1 = ((s32[4,1,512]{2,1,0:T(1,128)}), s32[4,1,512]{2,1,0:T(1,128)S(1)}, u32[]{:S(2)}, u32[]{:S(2)}) async-start(s32[4,1,512]{2,1,0:T(1,128)} %reshape.206), calls=%async_computation.1 | async-start | bytes 16384 | tf_op jit(solution)/shard_map/all_to_all | solution.py:52
  264.2 145.9 %all-to-all-start.3 = ((s32[8,4,32,2048]{3,2,0,1:T(8,128)}), s32[8,4,32,2048]{3,2,0,1:T(8,128)}, u32[]{:S(2)}, u32[]{:S(2)}) async-start(s32[8,4,32,2048]{3,2,0,1:T(8,128)} %copy.29), calls=%async_computation.3 | async-start | bytes 16777216 | tf_op jit(solution)/shard_map/all_to_all | solution.py:45
